TPU v7x, 32 devices: a whole 2x2x4 slice. The times are simulated.
32 devices in a mesh: dp: 4 (over x, y), tp: 8 (over z, core).
Axes of the slice: x: 2, y: 2, z: 4, core: 2. Of those that a mesh axis runs over, the one named last changes fastest.
Arguments:
- resid_in: bfloat16 [2048, 1024], P('dp'), parts along dimension 0
- cand_ids: int32 [2048, 256], P('dp'), parts along dimension 0
- ln_mlp: bfloat16 [1024], replicated
- wi_gate: bfloat16 [1024, 2816], P(None, 'tp')
- wi_lin: bfloat16 [1024, 2816], P(None, 'tp')
- w_out: bfloat16 [2816, 1024], P('tp')
- ln_final: bfloat16 [1024], replicated
- w_lm: bfloat16 [1024, 250112], P(None, 'tp')
Outputs:
- output 1: float32 [2048, 256], P('dp'), parts along dimension 0
- output 2: float32 [2048], P('dp'), parts along dimension 0
There are 4 independent parts. A program takes and returns all parts, laid end to end along the dimension named above; an argument that names none is the same for every part.
All inputs are finite; a program needn't handle non-finite values.
Results may differ from a plain program's by a relative error of at most 0.00164813.
Values sent between devices are 32-bit elements.
A program may use at most 1 GiB of HBM per device.

v0:
```python
import jax
import jax.numpy as jnp
from jax import lax
from jax.sharding import PartitionSpec as P

EPS = 1e-6


def rms_norm(values_in, scale_vec):
    wide = values_in.astype(jnp.float32)
    mean_sq = jnp.mean(wide * wide, axis=-1, keepdims=True)
    return (wide * lax.rsqrt(mean_sq + EPS) * scale_vec.astype(jnp.float32)).astype(jnp.bfloat16)


def solution(mesh):
    def local_step(resid_in, cand_ids, ln_mlp, wi_gate, wi_lin, w_out, ln_final, w_lm):
        normed = rms_norm(resid_in, ln_mlp)
        act_gate = jnp.dot(normed, wi_gate, preferred_element_type=jnp.float32)
        act_lin = jnp.dot(normed, wi_lin, preferred_element_type=jnp.float32)
        hidden = (jax.nn.gelu(act_gate, approximate=True) * act_lin).astype(jnp.bfloat16)
        part_out = jnp.dot(hidden, w_out, preferred_element_type=jnp.float32)
        mlp_out = lax.psum(part_out, "tp")
        resid_out = (resid_in.astype(jnp.float32) + mlp_out).astype(jnp.bfloat16)
        final_z = rms_norm(resid_out, ln_final)
        logits = jnp.dot(final_z, w_lm, preferred_element_type=jnp.float32)
        shard_cols = logits.shape[1]
        row_max = lax.pmax(jnp.max(logits, axis=-1), "tp")
        exp_sum = lax.psum(jnp.sum(jnp.exp(logits - row_max[:, None]), axis=-1), "tp")
        log_norm = row_max + jnp.log(exp_sum)
        local_ids = cand_ids - lax.axis_index("tp") * shard_cols
        is_owned = (local_ids >= 0) & (local_ids < shard_cols)
        picked = jnp.take_along_axis(logits, jnp.clip(local_ids, 0, shard_cols - 1), axis=1)
        cand_logits = lax.psum(jnp.where(is_owned, picked, 0.0), "tp")
        return cand_logits - log_norm[:, None], log_norm

    in_specs = (P("dp", None), P("dp", None), P(None), P(None, "tp"), P(None, "tp"), P("tp", None), P(None), P(None, "tp"))
    return jax.shard_map(local_step, mesh=mesh, in_specs=in_specs, out_specs=(P("dp", None), P("dp")), check_vma=False)
```

profile of v0, /device:TPU:0, one launch (start us, length us, event | category | flops | bytes accessed | tf_op | source)
XLA Modules:
  0.0 5689.9 jit_solution(5600022633273570567)
XLA Ops:
  7.2 0.0 copy-start
  7.2 0.0 copy-start.2
  7.2 0.0 copy-start.8
  7.2 0.0 all-reduce.3.cloned.1.call-start
  7.2 1.7 fusion.3
  8.9 0.7 convert_element_type.26
  9.6 2.1 fusion.28
  11.7 0.0 copy-done
  11.7 0.0 copy-done.2
  11.7 0.0 copy-done.8
  11.7 2.8 fusion.8
  14.5 0.0 copy-start.7
  14.5 0.0 copy-start.3
  14.5 0.0 all-reduce.3.cloned.1.call-update
  14.5 0.0 all-reduce.5.cloned.1.call-start
  14.6 0.6 copy-done.7
  15.2 0.4 copy-done.3
  15.5 0.3 fusion.21
  15.8 0.3 copy.10
  16.1 66.3 %all-reduce.3.cloned.1.call-done = f32[512,1024]{1,0:T(8,128)} async-done(((f32[512,1024]{1,0:T(8,128)}), f32[512,1024]{1,0:T(8,128)}) %all-reduce.3.cloned.1.call-update) | async-done | bytes 2097168 | tf_op jit(solution)/shard_map/psum | solution.py:22
  82.3 1.9 fusion
  84.3 55.7 fusion.35
  140.0 14.1 pmax.7
  154.1 0.0 copy-start.4
  154.1 3164.9 %gather_fusion = f32[131072]{0:T(1024)S(1)} fusion(f32[512,31264]{0,1:T(8,128)} %get-tuple-element.3, s32[131072]{0:T(1024)S(1)} %bitcast.13), kind=kCustom, calls=%fused_computation | custom fusion | bytes 2097152 | tf_op jit(solution)/shard_map/jit(take_along_axis)/gather | solution.py:32
  3319.0 0.0 copy-start.5
  3319.0 0.1 reshape.37
  3319.2 0.0 copy-done.4
  3319.2 1.1 select_select_fusion
  3320.3 0.0 all-reduce.5.cloned.1.call-update
  3320.3 0.0 copy-done.5
  3320.3 0.0 copy-start.1
  3320.3 20.3 exponential_reduce_fusion
  3340.6 2322.1 %psum.23 = f32[512]{0:T(512)S(1)} all-reduce(f32[512]{0:T(512)S(1)} %exponential_reduce_fusion), channel_id=1, replica_groups=mesh['dp'=4,'tp'=8] {'tp'}, use_global_device_ids=true, to_apply=%region_7.8 | all-reduce | flops 512 | bytes 4096 | tf_op jit(solution)/shard_map/psum | solution.py:28
  5662.7 0.0 copy-start.6
  5662.7 18.4 all-reduce.5.cloned.1.call-done
  5681.1 2.0 broadcast_subtract_fusion
  5683.1 0.0 copy-done.6
  5683.1 0.0 copy-done.1
  (4 shorter events, 0.0 us)
Async XLA Ops:
  7.2 4.5 copy-start
  7.2 4.5 copy-start.2
  7.2 4.5 copy-start.8
  7.2 75.1 %all-reduce.3.cloned.1.call-start = ((), (), s32[]{:S(2)}) async-start(), calls=%async_computation | async-start | bytes 4194304 | tf_op jit(solution)/shard_map/psum | solution.py:22
  14.5 0.7 copy-start.7
  14.5 1.1 copy-start.3
  14.5 5666.6 %all-reduce.5.cloned.1.call-start = ((), (), s32[]{:S(2)}) async-start(), calls=%async_computation.1 | async-start | bytes 1048576 | tf_op jit(solution)/shard_map/psum | solution.py:33
  154.1 3165.1 %copy-start.4 = (s32[512,256]{1,0:T(8,128)S(1)}, s32[512,256]{1,0:T(8,128)}, u32[]{:S(2)}) copy-start(s32[512,256]{1,0:T(8,128)} %param.9) | copy-start | bytes 1572868
  3319.0 1.3 copy-start.5
  3320.3 2362.8 %copy-start.1 = (bf16[352,1024]{1,0:T(8,128)(2,1)S(1)}, bf16[352,1024]{1,0:T(8,128)(2,1)}, u32[]{:S(2)}) copy-start(bf16[352,1024]{1,0:T(8,128)(2,1)} %param.13) | copy-start | bytes 2162692
  5662.7 20.4 copy-start.6
Sparse Core Ops, SparseCore 0:
  14.6 67.6 all-reduce.2
  3320.4 2360.6 all-reduce.4
where the time goes:
time: 5790 us; the launch traced here: 5690 us
  local copies, waits for them, and re-layouts  3170 us (55%)
  blocking collectives  2340 us (40%)
  waiting for transfers between devices  84.7 us (1%)
  matrix products  60.5 us (1%)
    gather x2, local copies, waits for them, and re-layouts, local_step(): jnp.take_along_axis(logits, jnp.clip(local_ids, 0, shard_cols - 1), axis=1)  3170 us
    psum x1, blocking collectives, local_step(): lax.psum(jnp.sum(jnp.exp(logits - row_max[:, None]), axis=-1), 'tp')  2320 us
  transfers between devices with their start and end apart: 2, of which 2 were waited for; matrix products, arithmetic and copies ran while one was open for 0% of the time, Pallas kernels for 0%

commit v1 on v0

v1 whole, which is shorter than its diff:
```python
import functools

import jax
import jax.numpy as jnp
from jax import lax
from jax.experimental import pallas as pl
from jax.experimental.pallas import tpu as pltpu
from jax.sharding import PartitionSpec as P

EPS = 1e-6
TILE = 2048
SLOTS = 3
ROW_GROUP = 8
LANES = 128
f32 = jnp.float32


def rms_norm(values_in, scale_vec):
    wide = values_in.astype(f32)
    mean_sq = jnp.mean(wide * wide, axis=-1, keepdims=True)
    return (wide * lax.rsqrt(mean_sq + EPS) * scale_vec.astype(f32)).astype(jnp.bfloat16)


def dot_t(a, b):
    return lax.dot_general(a, b, (((1,), (1,)), ((), ())), preferred_element_type=f32)


def absorb(logits, ncols, first_chunk, lane, chunk, top, total, picked, valid=None):
    nk = ncols // LANES
    for r in range(0, logits.shape[0], ROW_GROUP):
        rows = pl.ds(r, ROW_GROUP)
        parts = [logits[rows, LANES * k : LANES * (k + 1)] for k in range(nk)]
        for h in range(picked.shape[1] // LANES):
            cols = pl.ds(LANES * h, LANES)
            lanes_h, chunk_h, acc = lane[rows, cols], chunk[rows, cols], picked[rows, cols]
            for k in range(nk):
                got = jnp.take_along_axis(parts[k], lanes_h, axis=1, mode="promise_in_bounds")
                acc = jnp.where(chunk_h == first_chunk + k, got, acc)
            picked[rows, cols] = acc
        if valid is not None:
            col = lax.broadcasted_iota(jnp.int32, (ROW_GROUP, LANES), 1)
            parts = [p if LANES * (k + 1) <= valid else jnp.where(col < valid - LANES * k, p, -jnp.inf) for k, p in enumerate(parts) if LANES * k < valid]
        old = top[rows, :]
        new = functools.reduce(jnp.maximum, parts, old)
        terms = [jnp.exp(p - new) for p in parts]
        while len(terms) > 1:
            terms = [sum(terms[i : i + 2]) for i in range(0, len(terms), 2)]
        total[rows, :] = total[rows, :] * jnp.exp(old - new) + terms[0]
        top[rows, :] = new


def head_kernel(vocab, z, ids, w_hbm, picked, lse, wbuf, wtail, la, lb, lane, chunk, top, total, sems, tail_sem):
    full = vocab // TILE
    left = vocab - full * TILE
    padded = wtail.shape[0]

    def fetch(j, slot):
        return pltpu.make_async_copy(w_hbm.at[pl.ds(pl.multiple_of(j * TILE, TILE), TILE), :], wbuf.at[slot], sems.at[slot])

    for j in range(SLOTS):
        fetch(j, j).start()
    tail = pltpu.make_async_copy(w_hbm.at[pl.ds(full * TILE, left), :], wtail.at[pl.ds(0, left), :], tail_sem)
    tail.start()
    wtail[left:, :] = jnp.zeros((padded - left, wtail.shape[1]), jnp.bfloat16)
    local = ids[...]
    lane[...] = local & (LANES - 1)
    chunk[...] = jnp.where((local < 0) | (local >= vocab), -1, local >> 7)
    picked[...] = jnp.zeros_like(picked)
    top[...] = jnp.full_like(top, -jnp.inf)
    total[...] = jnp.zeros_like(total)

    bufs = (la, lb)
    fold = functools.partial(absorb, lane=lane, chunk=chunk, top=top, total=total, picked=picked)

    def multiply(j, slot, dst):
        fetch(j, slot).wait()
        dst[...] = dot_t(z[...], wbuf[slot])

    multiply(0, 0, la)

    def body(i, _):
        for u in range(2):
            j = 1 + 2 * i + u
            multiply(j, lax.rem(j, SLOTS), bufs[(1 + u) % 2])
            fold(bufs[u % 2], TILE, (j - 1) * (TILE // LANES))

            @pl.when(j - 1 + SLOTS < full)
            def _():
                fetch(j - 1 + SLOTS, lax.rem(j - 1, SLOTS)).start()

        return 0

    steps = (full - 1) // 2
    lax.fori_loop(0, steps, body, 0)
    j = 1 + 2 * steps
    while j < full:
        multiply(j, j % SLOTS, bufs[j % 2])
        fold(bufs[(j - 1) % 2], TILE, (j - 1) * (TILE // LANES))
        j += 1
    tail.wait()
    bufs[j % 2][:, 0:padded] = dot_t(z[...], wtail[...])
    fold(bufs[(j - 1) % 2], TILE, (j - 1) * (TILE // LANES))
    fold(bufs[j % 2], padded, j * (TILE // LANES), valid=left)
    high = jnp.max(top[...], axis=-1, keepdims=True)
    lse[...] = high + jnp.log(jnp.sum(total[...] * jnp.exp(top[...] - high), axis=-1, keepdims=True))


def head(z, local_ids, w_rows):
    rows, depth = z.shape
    cands = local_ids.shape[1]
    vocab = w_rows.shape[0]
    padded = -(-(vocab % TILE) // LANES) * LANES
    vmem = pl.BlockSpec(memory_space=pltpu.VMEM)
    return pl.pallas_call(
        functools.partial(head_kernel, vocab),
        out_shape=(jax.ShapeDtypeStruct((rows, cands), f32), jax.ShapeDtypeStruct((rows, 1), f32)),
        in_specs=[vmem, vmem, pl.BlockSpec(memory_space=pl.ANY)],
        out_specs=(vmem, vmem),
        scratch_shapes=[
            pltpu.VMEM((SLOTS, TILE, depth), jnp.bfloat16),
            pltpu.VMEM((padded, depth), jnp.bfloat16),
            pltpu.VMEM((rows, TILE), f32),
            pltpu.VMEM((rows, TILE), f32),
            pltpu.VMEM((rows, cands), jnp.int32),
            pltpu.VMEM((rows, cands), jnp.int32),
            pltpu.VMEM((rows, LANES), f32),
            pltpu.VMEM((rows, LANES), f32),
            pltpu.SemaphoreType.DMA((SLOTS,)),
            pltpu.SemaphoreType.DMA,
        ],
        compiler_params=pltpu.CompilerParams(vmem_limit_bytes=60 << 20),
        cost_estimate=pl.CostEstimate(flops=2 * rows * depth * vocab, bytes_accessed=2 * vocab * depth, transcendentals=rows * vocab),
        name="head",
    )(z, local_ids, w_rows)


def solution(mesh):
    n = mesh.shape["tp"]

    def local_step(resid_in, cand_ids, ln_mlp, wi_gate, wi_lin, w_out, ln_final, w_lm):
        normed = rms_norm(resid_in, ln_mlp)
        act_gate = jnp.dot(normed, wi_gate, preferred_element_type=f32)
        act_lin = jnp.dot(normed, wi_lin, preferred_element_type=f32)
        hidden = (jax.nn.gelu(act_gate, approximate=True) * act_lin).astype(jnp.bfloat16)
        mlp_out = lax.psum(jnp.dot(hidden, w_out, preferred_element_type=f32), "tp")
        resid_out = (resid_in.astype(f32) + mlp_out).astype(jnp.bfloat16)
        final_z = rms_norm(resid_out, ln_final)
        me = lax.axis_index("tp")
        picked, lse = head(final_z, cand_ids - me * w_lm.shape[1], w_lm.T)
        slots = jnp.where(lax.broadcasted_iota(jnp.int32, (1, n), 1) == me, lse, 0.0)
        both = lax.psum(jnp.concatenate([picked, slots], axis=1), "tp")
        shares = both[:, cand_ids.shape[1] :]
        high = jnp.max(shares, axis=-1, keepdims=True)
        log_norm = high + jnp.log(jnp.sum(jnp.exp(shares - high), axis=-1, keepdims=True))
        return both[:, : cand_ids.shape[1]] - log_norm, log_norm[:, 0]

    in_specs = (P("dp", None), P("dp", None), P(None), P(None, "tp"), P(None, "tp"), P("tp", None), P(None), P(None, "tp"))
    return jax.shard_map(local_step, mesh=mesh, in_specs=in_specs, out_specs=(P("dp", None), P("dp")), check_vma=False)
```

time: 5790 us -> 207 us (0.04); the launches traced: 5690 us -> 206 us
  local copies, waits for them, and re-layouts: 3170 us -> 1.13 us
  blocking collectives: 2340 us -> 0 us
    gather x2 -> x0, local copies, waits for them, and re-layouts: 3170 us -> none  [local_step(): jnp.take_along_axis(logits, jnp.clip(local_ids, 0, shard_cols - 1), axis=1)]
    psum x1 -> x0, blocking collectives: 2320 us -> none  [local_step(): lax.psum(jnp.sum(jnp.exp(logits - row_max[:, None]), axis=-1), 'tp')]
where the time goes in v1:
time: 207 us; the launch traced here: 206 us
  waiting for transfers between devices  123 us (59%)
  Pallas kernels  48.7 us (24%)
  other arithmetic  14.2 us (7%)
  between operations  14.1 us (7%)
  matrix products  4.77 us (2%)
    psum x1, waiting for transfers between devices, local_step(): mlp_out = lax.psum(jnp.dot(hidden, w_out, preferred_element_type=f32), 'tp')  66 us
    psum x1, waiting for transfers between devices, local_step(): both = lax.psum(jnp.concatenate([picked, slots], axis=1), 'tp')  57.2 us
    pallas_call x1, Pallas kernels, head(): pl.pallas_call(functools.partial(head_kernel, vocab), out_shape=(jax.Shap...  48.7 us
  transfers between devices with their start and end apart: 2, of which 2 were waited for; matrix products, arithmetic and copies ran while one was open for 0% of the time, Pallas kernels for 0%

profile of v1, /device:TPU:0, one launch (start us, length us, event | category | flops | bytes accessed | tf_op | source)
XLA Modules:
  0.0 206.2 jit_solution(4931155594616776383)
XLA Ops:
  7.2 0.0 copy-start
  7.2 0.0 copy-start.2
  7.2 0.0 copy-start.7
  7.2 0.0 all-reduce.3.cloned.1.call-start
  7.2 1.7 fusion.3
  8.9 0.7 convert_element_type.26
  9.6 2.1 %fusion.23 = f32[512,352]{0,1:T(8,128)S(1)} fusion(bf16[1024,352]{0,1:T(8,128)(2,1)} %param.11, bf16[512,1024]{1,0:T(8,128)(2,1)} %param.8, f32[1024]{0:T(1024)S(1)} %convert_element_type.26, f32[512]{0:T(512)S(1)} %add_rsqrt_fusion.1), kind=kOutput, calls=%fused_computation.29 | convolution fusion | flops 371195904 | bytes 2496512 | tf_op jit(solution)/shard_map/dot_general | solution.py:142
  11.7 0.0 copy-done
  11.7 0.0 copy-done.2
  11.7 0.0 copy-done.7
  11.7 2.7 %fusion.8 = f32[512,1024]{1,0:T(8,128)} fusion(bf16[352,1024]{1,0:T(8,128)(2,1)S(1)} %copy-done, bf16[1024,352]{0,1:T(8,128)(2,1)S(1)} %copy-done.7, f32[512,352]{0,1:T(8,128)S(1)} %fusion.23, bf16[512,1024]{1,0:T(8,128)(2,1)S(1)} %copy-done.2, f32[1024]{0:T(1024)S(1)} %convert_element_type.26, f32[512]{0:T(512)S(1)} %add_rsqrt_fusion.1), kind=kOutput, calls=%fused_computation.14 | convolution fusion | flops 742096896 | bytes 5314560 | tf_op jit(solution)/shard_map/dot_general | solution.py:145
  14.4 0.0 copy-start.6
  14.4 0.0 copy-start.4
  14.4 0.0 all-reduce.3.cloned.1.call-update
  14.4 0.0 all-reduce.5.cloned.1.call-start
  14.5 0.6 copy-done.6
  15.1 0.4 copy-done.4
  15.5 0.8 broadcast_subtract_fusion.ids
  16.3 66.0 %all-reduce.3.cloned.1.call-done = f32[512,1024]{1,0:T(8,128)} async-done(((f32[512,1024]{1,0:T(8,128)}), f32[512,1024]{1,0:T(8,128)}) %all-reduce.3.cloned.1.call-update) | async-done | bytes 2097168 | tf_op jit(solution)/shard_map/psum | solution.py:145
  82.3 0.0 copy-start.3
  82.3 2.1 %fusion = f32[512]{0:T(512)S(1)} fusion(f32[512,1024]{1,0:T(8,128)} %all-reduce.3.cloned.1.call-done, bf16[512,1024]{1,0:T(8,128)(2,1)S(1)} %copy-done.2), kind=kLoop, calls=%fused_computation.5 | loop fusion | flops 3145216 | bytes 3147776 | tf_op jit(solution)/shard_map/reduce_sum | solution.py:20
  84.4 0.1 copy-done.3
  84.5 1.4 fusion.2.z
  85.8 48.7 %head.1 = (f32[512,256]{1,0:T(8,128)}, f32[512,1]{1,0:T(8,128)}) custom-call(bf16[512,1024]{1,0:T(8,128)(2,1)} %fusion.2.z, s32[512,256]{1,0:T(8,128)} %broadcast_subtract_fusion.ids, bf16[31264,1024]{1,0:T(8,128)(2,1)} %bitcast.4), custom_call_target="tpu_custom_call" | custom-call | flops 32782680064 | bytes 64028672 | tf_op jit(solution)/shard_map/head/pallas_call | solution.py:114
  134.5 0.0 copy-start.1
  134.5 1.2 reduce
  135.7 0.1 broadcast_select_fusion
  135.8 2.0 pad_maximum_fusion
  137.8 0.0 all-reduce.5.cloned.1.call-update
  137.8 57.2 %all-reduce.5.cloned.1.call-done = f32[512,264]{1,0:T(8,128)} async-done(((f32[512,264]{1,0:T(8,128)}), f32[512,264]{1,0:T(8,128)}) %all-reduce.5.cloned.1.call-update) | async-done | bytes 540688 | tf_op jit(solution)/shard_map/psum | solution.py:151
  195.1 1.1 slice_reduce_fusion
  196.1 1.2 exponential_reduce_fusion
  197.4 0.0 copy-start.5
  197.4 2.0 slice_subtract_fusion
  199.3 0.0 copy-done.5
  199.3 0.0 copy-done.1
  (5 shorter events, 0.0 us)
Async XLA Ops:
  7.2 4.5 %copy-start = (bf16[352,1024]{1,0:T(8,128)(2,1)S(1)}, bf16[352,1024]{1,0:T(8,128)(2,1)}, u32[]{:S(2)}) copy-start(bf16[352,1024]{1,0:T(8,128)(2,1)} %param.13) | copy-start | bytes 2162692
  7.2 4.5 %copy-start.2 = (bf16[512,1024]{1,0:T(8,128)(2,1)S(1)}, bf16[512,1024]{1,0:T(8,128)(2,1)}, u32[]{:S(2)}) copy-start(bf16[512,1024]{1,0:T(8,128)(2,1)} %param.8) | copy-start | bytes 3145732
  7.2 4.5 %copy-start.7 = (bf16[1024,352]{0,1:T(8,128)(2,1)S(1)}, bf16[1024,352]{0,1:T(8,128)(2,1)}, u32[]{:S(2)}) copy-start(bf16[1024,352]{0,1:T(8,128)(2,1)} %param.12) | copy-start | bytes 2162692
  7.2 75.1 %all-reduce.3.cloned.1.call-start = ((), (), s32[]{:S(2)}) async-start(), calls=%async_computation | async-start | bytes 4194304 | tf_op jit(solution)/shard_map/psum | solution.py:145
  14.4 0.7 copy-start.6
  14.4 1.1 copy-start.4
  14.4 180.6 %all-reduce.5.cloned.1.call-start = ((), (), s32[]{:S(2)}) async-start(), calls=%async_computation.1 | async-start | bytes 1572864 | tf_op jit(solution)/shard_map/psum | solution.py:151
  82.3 2.2 %copy-start.3 = (f32[512,1024]{1,0:T(8,128)S(1)}, f32[512,1024]{1,0:T(8,128)}, u32[]{:S(2)}) copy-start(f32[512,1024]{1,0:T(8,128)} %all-reduce.3.cloned.1.call-done) | copy-start | bytes 6291460
  134.5 64.8 %copy-start.1 = (bf16[352,1024]{1,0:T(8,128)(2,1)S(1)}, bf16[352,1024]{1,0:T(8,128)(2,1)}, u32[]{:S(2)}) copy-start(bf16[352,1024]{1,0:T(8,128)(2,1)} %param.13) | copy-start | bytes 2162692
  197.4 2.0 copy-start.5
Sparse Core Ops, SparseCore 0:
  14.6 67.6 all-reduce.2
  138.0 57.0 all-reduce.4

commit v2 on v1

--- a/solution.py
+++ b/solution.py
@@ -13,12 +13,6 @@
 ROW_GROUP = 8
 LANES = 128
 f32 = jnp.float32
-
-
-def rms_norm(values_in, scale_vec):
-    wide = values_in.astype(f32)
-    mean_sq = jnp.mean(wide * wide, axis=-1, keepdims=True)
-    return (wide * lax.rsqrt(mean_sq + EPS) * scale_vec.astype(f32)).astype(jnp.bfloat16)
 
 
 def dot_t(a, b):
@@ -102,7 +96,8 @@
     fold(bufs[(j - 1) % 2], TILE, (j - 1) * (TILE // LANES))
     fold(bufs[j % 2], padded, j * (TILE // LANES), valid=left)
     high = jnp.max(top[...], axis=-1, keepdims=True)
-    lse[...] = high + jnp.log(jnp.sum(total[...] * jnp.exp(top[...] - high), axis=-1, keepdims=True))
+    value = high + jnp.log(jnp.sum(total[...] * jnp.exp(top[...] - high), axis=-1, keepdims=True))
+    lse[...] = jnp.transpose(jnp.broadcast_to(value, top.shape))[0:8, :]
 
 
 def head(z, local_ids, w_rows):
@@ -113,7 +108,7 @@
     vmem = pl.BlockSpec(memory_space=pltpu.VMEM)
     return pl.pallas_call(
         functools.partial(head_kernel, vocab),
-        out_shape=(jax.ShapeDtypeStruct((rows, cands), f32), jax.ShapeDtypeStruct((rows, 1), f32)),
+        out_shape=(jax.ShapeDtypeStruct((rows, cands), f32), jax.ShapeDtypeStruct((8, rows), f32)),
         in_specs=[vmem, vmem, pl.BlockSpec(memory_space=pl.ANY)],
         out_specs=(vmem, vmem),
         scratch_shapes=[
@@ -134,25 +129,238 @@
     )(z, local_ids, w_rows)
 
 
+def rms(wide, scale_row):
+    mean_sq = jnp.mean(wide * wide, axis=-1, keepdims=True)
+    return (wide * lax.rsqrt(mean_sq + EPS) * scale_row).astype(jnp.bfloat16)
+
+
+class Line:
+    def __init__(self, src, total, near, edge, mate, own, sems, step, span):
+        self.src, self.total, self.near, self.edge, self.mate, self.own = src, total, near, edge, mate, own
+        self.send, self.recv = sems
+        self.step, self.span = step, span
+        self.me = lax.axis_index("tp")
+        self.core = lax.rem(self.me, 2)
+        chip = lax.div(self.me, 2)
+        self.inner = (chip == 1) | (chip == 2)
+        self.outer = jnp.logical_not(self.inner)
+        self.sib = self.me + 1 - 2 * self.core
+        self.pair = jnp.where(lax.rem(chip, 2) == 0, self.me + 2, self.me - 2)
+        self.across = jnp.where(chip == 1, self.me + 2, self.me - 2)
+        self.chunks = src.shape[0] // (2 * step)
+
+    def rows(self, k, core):
+        per = self.span // (2 * self.step)
+        start = self.span * (k // per) + (self.span // 2) * core + self.step * (k % per)
+        return pl.ds(pl.multiple_of(start, self.step), self.step)
+
+    def slot(self, k):
+        return pl.ds(k * self.step, self.step)
+
+    def copy(self, hop, k, src, dst, target):
+        return pltpu.make_async_remote_copy(
+            src_ref=src, dst_ref=dst, send_sem=self.send.at[hop, k], recv_sem=self.recv.at[hop, k],
+            device_id={"tp": target}, device_id_type=pl.DeviceIdType.MESH)
+
+    def swap(self, k):
+        return self.copy(0, k, self.src.at[self.rows(k, 1 - self.core)], self.near.at[self.slot(k)], self.sib)
+
+    def inward(self, k):
+        return self.copy(1, k, self.own.at[self.slot(k)], self.edge.at[self.slot(k)], self.pair)
+
+    def cross(self, k):
+        return self.copy(2, k, self.own.at[self.slot(k)], self.mate.at[self.slot(k)], self.across)
+
+    def outward(self, k):
+        return self.copy(3, k, self.total.at[self.rows(k, self.core)], self.total.at[self.rows(k, self.core)], self.pair)
+
+    def share(self, k, core):
+        return self.copy(4, k, self.total.at[self.rows(k, core)], self.total.at[self.rows(k, core)], self.sib)
+
+    def mine(self, k):
+        self.swap(k).wait_recv()
+        return self.src[self.rows(k, self.core), :] + self.near[self.slot(k), :]
+
+    def outer_in(self, k):
+        self.own[self.slot(k), :] = self.mine(k)
+        self.inward(k).start()
+
+    def inner_in(self, k):
+        mine = self.mine(k)
+        self.inward(k).wait_recv()
+        self.own[self.slot(k), :] = mine + self.edge[self.slot(k), :]
+        self.cross(k).start()
+
+    def inner_out(self, k):
+        self.cross(k).wait_recv()
+        self.total[self.rows(k, self.core), :] = self.own[self.slot(k), :] + self.mate[self.slot(k), :]
+        self.outward(k).start()
+        self.share(k, self.core).start()
+
+    def outer_out(self, k):
+        self.outward(k).wait_recv()
+        self.share(k, self.core).start()
+
+    def run(self, after):
+        @pl.when(self.outer)
+        def _():
+            for k in range(self.chunks):
+                self.outer_in(k)
+            for k in range(self.chunks + 1):
+                if k < self.chunks:
+                    self.outer_out(k)
+                if k >= 1:
+                    after(k - 1)
+
+        @pl.when(self.inner)
+        def _():
+            for k in range(self.chunks + LAG + 1):
+                if k < self.chunks:
+                    self.inner_in(k)
+                if LAG <= k < self.chunks + LAG:
+                    self.inner_out(k - LAG)
+                if k >= LAG + 1:
+                    after(k - LAG - 1)
+
+    def finish(self, k):
+        self.share(k, 1 - self.core).wait_recv()
+
+    def drain(self):
+        for k in range(self.chunks):
+            self.swap(k).wait_send()
+            self.share(k, self.core).wait_send()
+
+            @pl.when(self.outer)
+            def _():
+                self.inward(k).wait_send()
+
+            @pl.when(self.inner)
+            def _():
+                self.cross(k).wait_send()
+                self.outward(k).wait_send()
+
+    def greet(self, barrier):
+        for other in (self.sib, self.pair):
+            pl.semaphore_signal(barrier, inc=1, device_id={"tp": other}, device_id_type=pl.DeviceIdType.MESH)
+
+        @pl.when(self.inner)
+        def _():
+            pl.semaphore_signal(barrier, inc=1, device_id={"tp": self.across}, device_id_type=pl.DeviceIdType.MESH)
+
+    def met(self, barrier):
+        @pl.when(self.outer)
+        def _():
+            pl.semaphore_wait(barrier, 2)
+
+        @pl.when(self.inner)
+        def _():
+            pl.semaphore_wait(barrier, 3)
+
+
+LAG = 2
+MLP_STEP = 32
+PICK_STEP = 64
+
+
+def line_scratch(rows, width, step):
+    half = pltpu.VMEM((rows // 2, width), f32)
+    sems = pltpu.SemaphoreType.DMA((5, rows // (2 * step)))
+    return [half, half, half, half, sems, sems]
+
+
+def mlp_kernel(x, scales, gate, lin, out, z, part, total, near, edge, mate, own, send, recv):
+    line = Line(part, total, near, edge, mate, own, (send, recv), MLP_STEP, part.shape[0] // 2)
+    barrier = pltpu.get_barrier_semaphore()
+    line.greet(barrier)
+    per = line.chunks // 2
+    for h in range(2):
+        rows = pl.ds(h * line.span, line.span)
+        normed = rms(x[rows, :].astype(f32), scales[0:1, :])
+        hidden = (jax.nn.gelu(dot_t(normed, gate[...]), approximate=True) * dot_t(normed, lin[...])).astype(jnp.bfloat16)
+        part[rows, :] = jnp.dot(hidden, out[...], preferred_element_type=f32)
+        if h == 0:
+            line.met(barrier)
+        for k in range(per * h, per * (h + 1)):
+            line.swap(k).start()
+
+    def normalise(k):
+        line.finish(k)
+        for core in range(2):
+            rows = line.rows(k, core)
+            mid = (x[rows, :].astype(f32) + total[rows, :]).astype(jnp.bfloat16)
+            z[rows, :] = rms(mid.astype(f32), scales[1:2, :])
+
+    line.run(normalise)
+    line.drain()
+
+
+def mlp(x, scales, gate, lin, out):
+    rows, width = x.shape
+    vmem = pl.BlockSpec(memory_space=pltpu.VMEM)
+    return pl.pallas_call(
+        mlp_kernel,
+        out_shape=jax.ShapeDtypeStruct(x.shape, jnp.bfloat16),
+        in_specs=[vmem] * 5,
+        out_specs=vmem,
+        scratch_shapes=[pltpu.VMEM((rows, width), f32), pltpu.VMEM((rows, width), f32)] + line_scratch(rows, width, MLP_STEP),
+        compiler_params=pltpu.CompilerParams(collective_id=0, has_side_effects=True, vmem_limit_bytes=48 << 20),
+        name="mlp",
+    )(x, scales, gate, lin, out)
+
+
+def merge_kernel(n, picked, lse, both, norm, shares, near, edge, mate, own, send, recv, ssend, srecv):
+    line = Line(picked, both, near, edge, mate, own, (send, recv), PICK_STEP, picked.shape[0])
+    barrier = pltpu.get_barrier_semaphore()
+    for d in range(1, n):
+        pl.semaphore_signal(barrier, inc=1, device_id={"tp": lax.rem(line.me + d, n)}, device_id_type=pl.DeviceIdType.MESH)
+    pl.semaphore_wait(barrier, n - 1)
+
+    def tell(d):
+        return pltpu.make_async_remote_copy(
+            src_ref=lse, dst_ref=shares.at[line.me], send_sem=ssend.at[d - 1], recv_sem=srecv.at[d - 1],
+            device_id={"tp": lax.rem(line.me + d, n)}, device_id_type=pl.DeviceIdType.MESH)
+
+    for k in range(line.chunks):
+        line.swap(k).start()
+    for d in range(1, n):
+        tell(d).start()
+    line.run(line.finish)
+    for d in range(1, n):
+        tell(d).wait_recv()
+    shares[line.me] = lse[...]
+    high = jnp.max(shares[...], axis=0)
+    acc = jnp.sum(jnp.exp(shares[...] - high), axis=0)
+    norm[...] = high + jnp.log(acc)
+    for d in range(1, n):
+        tell(d).wait_send()
+    line.drain()
+
+
+def merge(n, picked, lse):
+    rows, cands = picked.shape
+    vmem = pl.BlockSpec(memory_space=pltpu.VMEM)
+    return pl.pallas_call(
+        functools.partial(merge_kernel, n),
+        out_shape=(jax.ShapeDtypeStruct(picked.shape, f32), jax.ShapeDtypeStruct(lse.shape, f32)),
+        in_specs=[vmem] * 2,
+        out_specs=(vmem, vmem),
+        scratch_shapes=[pltpu.VMEM((n, *lse.shape), f32)] + line_scratch(rows, cands, PICK_STEP)
+        + [pltpu.SemaphoreType.DMA((n - 1,)), pltpu.SemaphoreType.DMA((n - 1,))],
+        compiler_params=pltpu.CompilerParams(collective_id=1, has_side_effects=True),
+        name="merge",
+    )(picked, lse)
+
+
 def solution(mesh):
     n = mesh.shape["tp"]
 
     def local_step(resid_in, cand_ids, ln_mlp, wi_gate, wi_lin, w_out, ln_final, w_lm):
-        normed = rms_norm(resid_in, ln_mlp)
-        act_gate = jnp.dot(normed, wi_gate, preferred_element_type=f32)
-        act_lin = jnp.dot(normed, wi_lin, preferred_element_type=f32)
-        hidden = (jax.nn.gelu(act_gate, approximate=True) * act_lin).astype(jnp.bfloat16)
-        mlp_out = lax.psum(jnp.dot(hidden, w_out, preferred_element_type=f32), "tp")
-        resid_out = (resid_in.astype(f32) + mlp_out).astype(jnp.bfloat16)
-        final_z = rms_norm(resid_out, ln_final)
-        me = lax.axis_index("tp")
-        picked, lse = head(final_z, cand_ids - me * w_lm.shape[1], w_lm.T)
-        slots = jnp.where(lax.broadcasted_iota(jnp.int32, (1, n), 1) == me, lse, 0.0)
-        both = lax.psum(jnp.concatenate([picked, slots], axis=1), "tp")
-        shares = both[:, cand_ids.shape[1] :]
-        high = jnp.max(shares, axis=-1, keepdims=True)
-        log_norm = high + jnp.log(jnp.sum(jnp.exp(shares - high), axis=-1, keepdims=True))
-        return both[:, : cand_ids.shape[1]] - log_norm, log_norm[:, 0]
+        scales = jnp.stack([ln_mlp, ln_final]).astype(f32)
+        z = mlp(resid_in, scales, wi_gate.T, wi_lin.T, w_out)
+        picked, lse = head(z, cand_ids - lax.axis_index("tp") * w_lm.shape[1], w_lm.T)
+        both, norm = merge(n, picked, lse)
+        log_norm = norm[0]
+        return both - log_norm[:, None], log_norm
 
     in_specs = (P("dp", None), P("dp", None), P(None), P(None, "tp"), P(None, "tp"), P("tp", None), P(None), P(None, "tp"))
     return jax.shard_map(local_step, mesh=mesh, in_specs=in_specs, out_specs=(P("dp", None), P("dp")), check_vma=False)

time: 207 us -> 125 us (0.60)
  waiting for transfers between devices: 123 us -> 0 us
  Pallas kernels: 48.7 us -> 112 us
  between operations: 14.1 us -> 0.68 us
  other arithmetic: 14.2 us -> 3.86 us
  local copies, waits for them, and re-layouts: 1.13 us -> 7.61 us
  matrix products: 4.77 us -> 0 us
    psum x2 -> x0, waiting for transfers between devices: 123 us -> none  [the longest x1 66 us: local_step(): mlp_out = lax.psum(jnp.dot(hidden, w_out, preferred_element_type=f32), 'tp')]
    pallas_call x0 -> x2, Pallas kernels: none -> 63.7 us  [the longest x1 40.6 us: mlp(): pl.pallas_call(mlp_kernel, out_shape=jax.ShapeDtypeStruct(x.shape, jnp.bf...]
    reduce_sum x3 -> x0, other arithmetic: 4.93 us -> none  [the longest x2 3.74 us: rms_norm(): mean_sq = jnp.mean(wide * wide, axis=-1, keepdims=True)]
    dot_general x2 -> x0, matrix products: 4.77 us -> none  [the longest x1 2.71 us: local_step(): mlp_out = lax.psum(jnp.dot(hidden, w_out, preferred_element_type=f32), 'tp')]
    unnamed x16 -> x12, local copies, waits for them, and re-layouts: 1.13 us -> 5.52 us
  transfers between devices with their start and end apart: 2 -> 0, of which waited for: 2 -> 0; matrix products, arithmetic and copies ran while one was open for 0% -> 0% of each run, Pallas kernels for 0% -> 0%
where the time goes in v2:
time: 125 us; the launch traced here: 124 us
  Pallas kernels  112 us (90%)
  local copies, waits for them, and re-layouts  7.61 us (6%)
  other arithmetic  3.86 us (3%)
    pallas_call x1, Pallas kernels, head(): pl.pallas_call(functools.partial(head_kernel, vocab), out_shape=(jax.Shap...  48.4 us
    pallas_call x1, Pallas kernels, mlp(): pl.pallas_call(mlp_kernel, out_shape=jax.ShapeDtypeStruct(x.shape, jnp.bf...  40.6 us
    pallas_call x1, Pallas kernels, merge(): pl.pallas_call(functools.partial(merge_kernel, n), out_shape=(jax.ShapeDt...  23.1 us
    unnamed x12, local copies, waits for them, and re-layouts  5.52 us

profile of v2, /device:TPU:0, one launch (start us, length us, event | category | flops | bytes accessed | tf_op | source)
XLA Modules:
  0.0 124.2 jit_solution(3807619921537451637)
XLA Ops:
  0.6 0.7 stack.9
  1.3 0.7 stack.10
  2.0 1.9 %broadcast_subtract_fusion.1.ids = s32[512,256]{1,0:T(8,128)} fusion(s32[512,256]{1,0:T(8,128)} %param.9, s32[]{:T(128)S(6)} %mul.3), kind=kLoop, calls=%fused_computation.1 | loop fusion | flops 131072 | bytes 1048580 | tf_op jit(solution)/shard_map/sub | solution.py:360
  3.9 0.0 copy-start
  3.9 1.2 copy-done
  5.1 0.0 copy-start.2
  5.1 1.1 copy-done.2
  6.2 0.0 copy-start.3
  6.2 1.1 copy-done.3
  7.3 0.0 copy-start.4
  7.3 1.1 copy-done.4
  8.5 40.6 %mlp.1.z = bf16[512,1024]{1,0:T(8,128)(2,1)S(1)} custom-call(bf16[512,1024]{1,0:T(8,128)(2,1)S(1)} %copy-done, f32[2,1024]{1,0:T(2,128)S(1)} %maximum_convert_fusion.scales, bf16[352,1024]{1,0:T(8,128)(2,1)S(1)} %bitcast.4, bf16[352,1024]{1,0:T(8,128)(2,1)S(1)} %bitcast.5, bf16[352,1024]{1,0:T(8,128)(2,1)S(1)} %copy-done.4), custom_call_target="tpu_custom_call" | custom-call | tf_op jit(solution)/shard_map/mlp/pallas_call | solution.py:300
  49.1 0.0 copy-start.1
  49.1 1.0 copy-done.1
  50.1 48.4 %head.1 = (f32[512,256]{1,0:T(8,128)}, f32[8,512]{1,0:T(8,128)}) custom-call(bf16[512,1024]{1,0:T(8,128)(2,1)} %copy-done.1, s32[512,256]{1,0:T(8,128)} %broadcast_subtract_fusion.1.ids, bf16[31264,1024]{1,0:T(8,128)(2,1)} %bitcast.8), custom_call_target="tpu_custom_call" | custom-call | flops 32782680064 | bytes 64028672 | tf_op jit(solution)/shard_map/head/pallas_call | solution.py:109
  98.5 23.1 %merge.1 = (f32[512,256]{1,0:T(8,128)}, f32[8,512]{1,0:T(8,128)}) custom-call(f32[512,256]{1,0:T(8,128)} %get-tuple-element.6.picked, f32[8,512]{1,0:T(8,128)} %get-tuple-element.7.lse), custom_call_target="tpu_custom_call" | custom-call | tf_op jit(solution)/shard_map/merge/pallas_call | solution.py:342
  121.5 0.7 slice.3
  122.3 0.0 copy-start.5
  122.3 2.0 %broadcast_subtract_fusion = f32[512,256]{1,0:T(8,128)} fusion(f32[512,256]{1,0:T(8,128)} %get-tuple-element.8, f32[512]{0:T(512)S(1)} %bitcast.6), kind=kLoop, calls=%fused_computation | loop fusion | flops 131072 | bytes 1050624 | tf_op jit(solution)/shard_map/sub | solution.py:363
  124.2 0.0 copy-done.5
  (1 shorter events, 0.0 us)
Async XLA Ops:
  3.9 1.2 copy-start
  5.1 1.1 copy-start.2
  6.2 1.1 copy-start.3
  7.3 1.1 copy-start.4
  49.1 1.0 copy-start.1
  122.3 2.0 %copy-start.5 = (f32[1,512]{1,0:T(1,128)}, f32[1,512]{1,0:T(1,128)S(1)}, u32[]{:S(2)}) copy-start(f32[1,512]{1,0:T(1,128)S(1)} %slice.3) | copy-start | bytes 6148

commit v3 on v2

--- a/solution.py
+++ b/solution.py
@@ -43,7 +43,7 @@
         top[rows, :] = new
 
 
-def head_kernel(vocab, z, ids, w_hbm, picked, lse, wbuf, wtail, la, lb, lane, chunk, top, total, sems, tail_sem):
+def head_kernel(vocab, z_in, ids_in, w_hbm, picked, lse, z, ids, in_sems, wbuf, wtail, la, lb, lane, chunk, top, total, sems, tail_sem):
     full = vocab // TILE
     left = vocab - full * TILE
     padded = wtail.shape[0]
@@ -51,12 +51,17 @@
     def fetch(j, slot):
         return pltpu.make_async_copy(w_hbm.at[pl.ds(pl.multiple_of(j * TILE, TILE), TILE), :], wbuf.at[slot], sems.at[slot])
 
+    loads = [pltpu.make_async_copy(z_in, z, in_sems.at[0]), pltpu.make_async_copy(ids_in, ids, in_sems.at[1])]
+    for load in loads:
+        load.start()
     for j in range(SLOTS):
         fetch(j, j).start()
     tail = pltpu.make_async_copy(w_hbm.at[pl.ds(full * TILE, left), :], wtail.at[pl.ds(0, left), :], tail_sem)
     tail.start()
     wtail[left:, :] = jnp.zeros((padded - left, wtail.shape[1]), jnp.bfloat16)
-    local = ids[...]
+    for load in loads:
+        load.wait()
+    local = ids[...] - lax.axis_index("tp") * vocab
     lane[...] = local & (LANES - 1)
     chunk[...] = jnp.where((local < 0) | (local >= vocab), -1, local >> 7)
     picked[...] = jnp.zeros_like(picked)
@@ -100,18 +105,21 @@
     lse[...] = jnp.transpose(jnp.broadcast_to(value, top.shape))[0:8, :]
 
 
-def head(z, local_ids, w_rows):
+def head(z, ids, w_rows):
     rows, depth = z.shape
-    cands = local_ids.shape[1]
+    cands = ids.shape[1]
     vocab = w_rows.shape[0]
     padded = -(-(vocab % TILE) // LANES) * LANES
     vmem = pl.BlockSpec(memory_space=pltpu.VMEM)
     return pl.pallas_call(
         functools.partial(head_kernel, vocab),
         out_shape=(jax.ShapeDtypeStruct((rows, cands), f32), jax.ShapeDtypeStruct((8, rows), f32)),
-        in_specs=[vmem, vmem, pl.BlockSpec(memory_space=pl.ANY)],
+        in_specs=[pl.BlockSpec(memory_space=pl.ANY)] * 3,
         out_specs=(vmem, vmem),
         scratch_shapes=[
+            pltpu.VMEM(z.shape, z.dtype),
+            pltpu.VMEM(ids.shape, ids.dtype),
+            pltpu.SemaphoreType.DMA((2,)),
             pltpu.VMEM((SLOTS, TILE, depth), jnp.bfloat16),
             pltpu.VMEM((padded, depth), jnp.bfloat16),
             pltpu.VMEM((rows, TILE), f32),
@@ -123,10 +131,10 @@
             pltpu.SemaphoreType.DMA((SLOTS,)),
             pltpu.SemaphoreType.DMA,
         ],
-        compiler_params=pltpu.CompilerParams(vmem_limit_bytes=60 << 20),
+        compiler_params=pltpu.CompilerParams(vmem_limit_bytes=62 << 20),
         cost_estimate=pl.CostEstimate(flops=2 * rows * depth * vocab, bytes_accessed=2 * vocab * depth, transcendentals=rows * vocab),
         name="head",
-    )(z, local_ids, w_rows)
+    )(z, ids, w_rows)
 
 
 def rms(wide, scale_row):
@@ -257,9 +265,10 @@
             pl.semaphore_wait(barrier, 3)
 
 
-LAG = 2
-MLP_STEP = 32
-PICK_STEP = 64
+LAG = 3
+MLP_STEP = 16
+PICK_STEP = 32
+MERGE_LAG = 3
 
 
 def line_scratch(rows, width, step):
@@ -268,15 +277,23 @@
     return [half, half, half, half, sems, sems]
 
 
-def mlp_kernel(x, scales, gate, lin, out, z, part, total, near, edge, mate, own, send, recv):
+def mlp_kernel(x_in, scales, gate_in, lin_in, out_in, z, x, gate, lin, out, in_sems, part, total, near, edge, mate, own, send, recv):
     line = Line(part, total, near, edge, mate, own, (send, recv), MLP_STEP, part.shape[0] // 2)
     barrier = pltpu.get_barrier_semaphore()
     line.greet(barrier)
+    loads = [pltpu.make_async_copy(src, dst, in_sems.at[i]) for i, (src, dst) in enumerate(
+        ((x_in, x), (gate_in, gate), (lin_in, lin), (out_in, out)))]
+    for load in loads:
+        load.start()
+    for load in loads[:3]:
+        load.wait()
     per = line.chunks // 2
     for h in range(2):
         rows = pl.ds(h * line.span, line.span)
         normed = rms(x[rows, :].astype(f32), scales[0:1, :])
         hidden = (jax.nn.gelu(dot_t(normed, gate[...]), approximate=True) * dot_t(normed, lin[...])).astype(jnp.bfloat16)
+        if h == 0:
+            loads[3].wait()
         part[rows, :] = jnp.dot(hidden, out[...], preferred_element_type=f32)
         if h == 0:
             line.met(barrier)
@@ -297,42 +314,109 @@
 def mlp(x, scales, gate, lin, out):
     rows, width = x.shape
     vmem = pl.BlockSpec(memory_space=pltpu.VMEM)
+    hbm = pl.BlockSpec(memory_space=pl.ANY)
     return pl.pallas_call(
         mlp_kernel,
         out_shape=jax.ShapeDtypeStruct(x.shape, jnp.bfloat16),
-        in_specs=[vmem] * 5,
+        in_specs=[hbm, vmem, hbm, hbm, hbm],
         out_specs=vmem,
-        scratch_shapes=[pltpu.VMEM((rows, width), f32), pltpu.VMEM((rows, width), f32)] + line_scratch(rows, width, MLP_STEP),
-        compiler_params=pltpu.CompilerParams(collective_id=0, has_side_effects=True, vmem_limit_bytes=48 << 20),
+        scratch_shapes=[pltpu.VMEM(a.shape, a.dtype) for a in (x, gate, lin, out)] + [pltpu.SemaphoreType.DMA((4,))]
+        + [pltpu.VMEM((rows, width), f32), pltpu.VMEM((rows, width), f32)] + line_scratch(rows, width, MLP_STEP),
+        compiler_params=pltpu.CompilerParams(collective_id=0, has_side_effects=True, vmem_limit_bytes=62 << 20),
         name="mlp",
     )(x, scales, gate, lin, out)
 
 
-def merge_kernel(n, picked, lse, both, norm, shares, near, edge, mate, own, send, recv, ssend, srecv):
+class Slots:
+    def __init__(self, line, own, recv_buf, sems):
+        self.line, self.own, self.buf = line, own, recv_buf
+        self.send, self.recv = sems
+
+    def copy(self, hop, src, dst, target):
+        return pltpu.make_async_remote_copy(
+            src_ref=self.own.at[src], dst_ref=self.buf.at[dst], send_sem=self.send.at[hop], recv_sem=self.recv.at[hop],
+            device_id={"tp": target}, device_id_type=pl.DeviceIdType.MESH)
+
+    def hop(self, i):
+        line = self.line
+        return self.copy(i, i, i, (line.sib, line.pair, line.across, line.pair)[i])
+
+    def begin(self, mine):
+        self.own[0, :, :] = mine
+        self.hop(0).start()
+
+    def inner_in(self):
+        self.hop(0).wait_recv()
+        self.hop(1).wait_recv()
+        self.own[2, :, :] = self.own[0] + self.buf[0] + self.buf[1]
+        self.hop(2).start()
+
+    def inner_out(self):
+        self.hop(2).wait_recv()
+        self.own[3, :, :] = self.own[2] + self.buf[2]
+        self.hop(3).start()
+
+    def outer_in(self):
+        self.hop(0).wait_recv()
+        self.own[1, :, :] = self.own[0] + self.buf[0]
+        self.hop(1).start()
+
+    def outer_out(self):
+        self.hop(3).wait_recv()
+        self.own[3, :, :] = self.buf[3]
+
+    def drain(self):
+        self.hop(0).wait_send()
+
+        @pl.when(self.line.outer)
+        def _():
+            self.hop(1).wait_send()
+
+        @pl.when(self.line.inner)
+        def _():
+            self.hop(2).wait_send()
+            self.hop(3).wait_send()
+
+
+def merge_kernel(picked, lse, both, norm, mine, got, ssend, srecv, near, edge, mate, own, send, recv):
     line = Line(picked, both, near, edge, mate, own, (send, recv), PICK_STEP, picked.shape[0])
+    slots = Slots(line, mine, got, (ssend, srecv))
     barrier = pltpu.get_barrier_semaphore()
-    for d in range(1, n):
-        pl.semaphore_signal(barrier, inc=1, device_id={"tp": lax.rem(line.me + d, n)}, device_id_type=pl.DeviceIdType.MESH)
-    pl.semaphore_wait(barrier, n - 1)
-
-    def tell(d):
-        return pltpu.make_async_remote_copy(
-            src_ref=lse, dst_ref=shares.at[line.me], send_sem=ssend.at[d - 1], recv_sem=srecv.at[d - 1],
-            device_id={"tp": lax.rem(line.me + d, n)}, device_id_type=pl.DeviceIdType.MESH)
-
+    line.greet(barrier)
+    line.met(barrier)
     for k in range(line.chunks):
         line.swap(k).start()
-    for d in range(1, n):
-        tell(d).start()
-    line.run(line.finish)
-    for d in range(1, n):
-        tell(d).wait_recv()
-    shares[line.me] = lse[...]
-    high = jnp.max(shares[...], axis=0)
-    acc = jnp.sum(jnp.exp(shares[...] - high), axis=0)
-    norm[...] = high + jnp.log(acc)
-    for d in range(1, n):
-        tell(d).wait_send()
+    sub = lax.broadcasted_iota(jnp.int32, lse.shape, 0)
+    slots.begin(jnp.where(sub == line.me, lse[...], 0.0))
+
+    @pl.when(line.outer)
+    def _():
+        for k in range(line.chunks):
+            line.outer_in(k)
+        slots.outer_in()
+        for k in range(line.chunks):
+            line.outer_out(k)
+        slots.outer_out()
+
+    @pl.when(line.inner)
+    def _():
+        for k in range(line.chunks + 1):
+            if k < line.chunks:
+                line.inner_in(k)
+            else:
+                slots.inner_in()
+            if k >= MERGE_LAG:
+                line.inner_out(k - MERGE_LAG)
+        for k in range(line.chunks + 1 - MERGE_LAG, line.chunks):
+            line.inner_out(k)
+        slots.inner_out()
+
+    every = mine[3, :, :]
+    high = jnp.max(every, axis=0, keepdims=True)
+    norm[...] = jnp.broadcast_to(high + jnp.log(jnp.sum(jnp.exp(every - high), axis=0, keepdims=True)), norm.shape)
+    for k in range(line.chunks):
+        line.finish(k)
+    slots.drain()
     line.drain()
 
 
@@ -340,12 +424,13 @@
     rows, cands = picked.shape
     vmem = pl.BlockSpec(memory_space=pltpu.VMEM)
     return pl.pallas_call(
-        functools.partial(merge_kernel, n),
+        merge_kernel,
         out_shape=(jax.ShapeDtypeStruct(picked.shape, f32), jax.ShapeDtypeStruct(lse.shape, f32)),
         in_specs=[vmem] * 2,
         out_specs=(vmem, vmem),
-        scratch_shapes=[pltpu.VMEM((n, *lse.shape), f32)] + line_scratch(rows, cands, PICK_STEP)
-        + [pltpu.SemaphoreType.DMA((n - 1,)), pltpu.SemaphoreType.DMA((n - 1,))],
+        scratch_shapes=[pltpu.VMEM((4, *lse.shape), f32), pltpu.VMEM((4, *lse.shape), f32),
+                        pltpu.SemaphoreType.DMA((4,)), pltpu.SemaphoreType.DMA((4,))]
+        + line_scratch(rows, cands, PICK_STEP),
         compiler_params=pltpu.CompilerParams(collective_id=1, has_side_effects=True),
         name="merge",
     )(picked, lse)
@@ -357,7 +442,7 @@
     def local_step(resid_in, cand_ids, ln_mlp, wi_gate, wi_lin, w_out, ln_final, w_lm):
         scales = jnp.stack([ln_mlp, ln_final]).astype(f32)
         z = mlp(resid_in, scales, wi_gate.T, wi_lin.T, w_out)
-        picked, lse = head(z, cand_ids - lax.axis_index("tp") * w_lm.shape[1], w_lm.T)
+        picked, lse = head(z, cand_ids, w_lm.T)
         both, norm = merge(n, picked, lse)
         log_norm = norm[0]
         return both - log_norm[:, None], log_norm

time: 125 us -> 117 us (0.936)
  local copies, waits for them, and re-layouts: 7.61 us -> 2.1 us
  other arithmetic: 3.86 us -> 2.58 us
    unnamed x12 -> x2, local copies, waits for them, and re-layouts: 5.52 us -> 0.01 us
    pallas_call x1, Pallas kernels: 23.1 us -> 20 us  [merge(): pl.pallas_call(merge_kernel, out_shape=(jax.ShapeDtypeStruct(picked.shape...]
    sub x1 -> x0, other arithmetic: 1.87 us -> none  [local_step(): cand_ids - lax.axis_index('tp') * w_lm.shape[1]]
    pallas_call x1, Pallas kernels: 40.6 us -> 42.4 us  [mlp(): pl.pallas_call(mlp_kernel, out_shape=jax.ShapeDtypeStruct(x.shape, jnp.bf...]
where the time goes in v3:
time: 117 us
  Pallas kernels  112 us (96%)
  other arithmetic  2.58 us (2%)
  local copies, waits for them, and re-layouts  2.1 us (2%)
    pallas_call x1, Pallas kernels, head(): pl.pallas_call(functools.partial(head_kernel, vocab), out_shape=(jax.Shap...  49.1 us
    pallas_call x1, Pallas kernels, mlp(): pl.pallas_call(mlp_kernel, out_shape=jax.ShapeDtypeStruct(x.shape, jnp.bf...  42.4 us
    pallas_call x1, Pallas kernels, merge(): pl.pallas_call(merge_kernel, out_shape=(jax.ShapeDtypeStruct(picked.shape...  20 us

profile of v3, /device:TPU:0, one launch (start us, length us, event | category | flops | bytes accessed | tf_op | source)
XLA Modules:
  0.0 116.9 jit_solution(9103759200074437958)
XLA Ops:
  0.6 0.7 stack.9
  1.3 0.7 stack.10
  2.0 0.6 maximum_convert_fusion.scales
  2.6 42.4 %mlp.1.z_in = bf16[512,1024]{1,0:T(8,128)(2,1)} custom-call(bf16[512,1024]{1,0:T(8,128)(2,1)} %x_in.1, f32[2,1024]{1,0:T(2,128)} %maximum_convert_fusion.scales, bf16[352,1024]{1,0:T(8,128)(2,1)} %bitcast.4, bf16[352,1024]{1,0:T(8,128)(2,1)} %bitcast.5, bf16[352,1024]{1,0:T(8,128)(2,1)} %out_in.1), custom_call_target="tpu_custom_call" | custom-call | tf_op jit(solution)/shard_map/mlp/pallas_call | solution.py:318
  45.0 49.1 %head.1 = (f32[512,256]{1,0:T(8,128)}, f32[8,512]{1,0:T(8,128)}) custom-call(bf16[512,1024]{1,0:T(8,128)(2,1)} %mlp.1.z_in, s32[512,256]{1,0:T(8,128)} %ids_in.1, bf16[31264,1024]{1,0:T(8,128)(2,1)} %bitcast.8), custom_call_target="tpu_custom_call" | custom-call | flops 32782680064 | bytes 64028672 | tf_op jit(solution)/shard_map/head/pallas_call | solution.py:114
  94.1 20.0 %merge.1 = (f32[512,256]{1,0:T(8,128)}, f32[8,512]{1,0:T(8,128)}) custom-call(f32[512,256]{1,0:T(8,128)} %get-tuple-element.6.picked, f32[8,512]{1,0:T(8,128)} %get-tuple-element.7.lse), custom_call_target="tpu_custom_call" | custom-call | tf_op jit(solution)/shard_map/merge/pallas_call | solution.py:426
  114.2 0.7 slice.3
  114.9 0.0 copy-start
  114.9 2.0 %broadcast_subtract_fusion = f32[512,256]{1,0:T(8,128)} fusion(f32[512,256]{1,0:T(8,128)} %get-tuple-element.8, f32[512]{0:T(512)S(1)} %bitcast.6), kind=kLoop, calls=%fused_computation | loop fusion | flops 131072 | bytes 1050624 | tf_op jit(solution)/shard_map/sub | solution.py:448
  116.9 0.0 copy-done
Async XLA Ops:
  114.9 2.0 %copy-start = (f32[1,512]{1,0:T(1,128)}, f32[1,512]{1,0:T(1,128)S(1)}, u32[]{:S(2)}) copy-start(f32[1,512]{1,0:T(1,128)S(1)} %slice.3) | copy-start | bytes 6148
